TPU v7x, 32 devices: a whole 2x2x4 slice. The times are simulated.
32 devices in a mesh: pair: 2 (over y), dp: 8 (over z, x), ep: 2 (over core).
Axes of the slice: x: 2, y: 2, z: 4, core: 2. Of those that a mesh axis runs over, the one named last changes fastest.
Arguments:
- activations: bfloat16 [12288, 1024], P(('pair', 'dp'), 'ep'), parts along dimension 1, may hold values from -6 to 6
- cotangents: bfloat16 [12288, 4096], P(('pair', 'dp'), 'ep'), parts along dimension 1, may hold values from -0.875 to 0.875
Outputs:
- averaged_grad: bfloat16 [512, 4096], P('pair', 'ep'), parts along dimension 1
There are 2 independent parts, one for each index of `ep`. A program takes and returns all parts, laid end to end along the dimension named above; each array names one. Nothing has to cross between parts.
All inputs are finite; a program needn't handle non-finite values.
Results may differ from a plain program's by a relative error of at most 0.001.
Values may be sent and summed in bfloat16 or wider, within the bound.
A program may use at most 64 MiB of HBM per device.

v0:
```python
import functools

import jax
import jax.numpy as jnp
from jax import lax
from jax.experimental import pallas as pl
from jax.experimental.pallas import tpu as pltpu
from jax.sharding import PartitionSpec as P

LANES = 128
SPLIT = 2
AHEAD = 3
CROSS = 2
LAG = (4, 7, 10)


def kernel(np_, nx, nz, nc, ns, act_hbm, cot_hbm, out_ref, act_ref, cot_ref, act_t, part, f1, f2, zr,
           s1, r1, s2, r2, sz, rz, sg, rg, sx, rx, load):
    p = lax.axis_index("pair")
    dp = lax.axis_index("dp")
    z, x = dp // nx, dp % nx
    rs = part.shape[-2]
    chunks = nc * ns
    rows_p = nz * ns * rs
    cols_x = nc * LANES

    def other(i, q, n):
        return lax.rem(i + q, n)

    def to_pair(q):
        return {"pair": other(p, q, np_)}

    def to_x(q):
        return {"dp": z * nx + other(x, q, nx)}

    def to_z(q):
        return {"dp": other(z, q, nz) * nx + x}

    def crossed(k):
        return lax.rem(k, CROSS) == CROSS - 1

    def remote(src, dst, ssem, rsem, peer):
        return pltpu.make_async_remote_copy(
            src_ref=src, dst_ref=dst, send_sem=ssem, recv_sem=rsem,
            device_id=peer, device_id_type=pl.DeviceIdType.MESH)

    def first_a(k, q):
        return remote(part.at[k, other(p, q, np_)], f1.at[k, pl.ds(p * nx, nx)],
                      s1.at[k, q], r1.at[k, p], to_pair(q))

    def first_b(k, q):
        return remote(part.at[k, :, other(x, q, nx)], f1.at[k, pl.ds(x * np_, np_)],
                      s1.at[k, q], r1.at[k, x], to_x(q))

    def second_a(k, q):
        return remote(part.at[k, p, other(x, q, nx)], f2.at[k, x], s2.at[k, q], r2.at[k, x], to_x(q))

    def second_b(k, q):
        return remote(part.at[k, other(p, q, np_), x], f2.at[k, p], s2.at[k, q], r2.at[k, p], to_pair(q))

    def along_z(k, q):
        return remote(part.at[k, p, x, other(z, q, nz)], zr.at[k, z], sz.at[k, q], rz.at[k, z], to_z(q))

    def piece(k, zi, xi):
        c, s = k // ns, lax.rem(k, ns)
        row = pl.multiple_of((zi * ns + s) * rs, rs)
        col = pl.multiple_of(xi * cols_x + c * LANES, LANES)
        return out_ref.at[pl.ds(row, rs), pl.ds(col, LANES)]

    def gather_z(k, q):
        here = piece(k, z, x)
        return remote(here, here, sg.at[k, q], rg.at[k, z], to_z(q))

    def gather_x(k, zo, q):
        zi = other(z, zo, nz)
        here = piece(k, zi, x)
        return remote(here, here, sx.at[k, zi, q], rx.at[k, zi, x], to_x(q))

    def arrived(dst, ssem, rsem):
        remote(dst, dst, ssem, rsem, to_pair(1)).wait_recv()

    def start_first(k):
        @pl.when(crossed(k))
        def _():
            for q in range(1, nx):
                first_b(k, q).start()

        @pl.when(jnp.logical_not(crossed(k)))
        def _():
            for q in range(1, np_):
                first_a(k, q).start()

    def stage2(k):
        @pl.when(jnp.logical_not(crossed(k)))
        def _():
            for q in range(1, np_):
                o = other(p, q, np_)
                arrived(f1.at[k, pl.ds(o * nx, nx)], s1.at[k, q], r1.at[k, o])
                for i in range(nx):
                    part[k, p, i] += f1[k, o * nx + i]
            for q in range(1, nx):
                second_a(k, q).start()

        @pl.when(crossed(k))
        def _():
            for q in range(1, nx):
                o = other(x, q, nx)
                arrived(f1.at[k, pl.ds(o * np_, np_)], s1.at[k, q], r1.at[k, o])
                for i in range(np_):
                    part[k, i, x] += f1[k, o * np_ + i]
            for q in range(1, np_):
                second_b(k, q).start()

    def stage3(k):
        @pl.when(jnp.logical_not(crossed(k)))
        def _():
            for q in range(1, nx):
                o = other(x, q, nx)
                arrived(f2.at[k, o], s2.at[k, q], r2.at[k, o])
                part[k, p, x] += f2[k, o]

        @pl.when(crossed(k))
        def _():
            for q in range(1, np_):
                o = other(p, q, np_)
                arrived(f2.at[k, o], s2.at[k, q], r2.at[k, o])
                part[k, p, x] += f2[k, o]

        for q in range(1, nz):
            along_z(k, q).start()

    def stage4(k):
        total = part[k, p, x, z]
        for q in range(1, nz):
            o = other(z, q, nz)
            arrived(zr.at[k, o], sz.at[k, q], rz.at[k, o])
            total = total + zr[k, o]
        replicas = np_ * nx * nz
        piece(k, z, x)[...] = (total / replicas).astype(out_ref.dtype)
        for q in range(1, nz):
            gather_z(k, q).start()
        for q in range(1, nx):
            gather_x(k, 0, q).start()

    def stage5(k):
        for zo in range(1, nz):
            o = other(z, zo, nz)
            arrived(piece(k, o, x), sg.at[k, zo], rg.at[k, o])
            for q in range(1, nx):
                gather_x(k, zo, q).start()

    def stage6(k):
        for zi in range(nz):
            for q in range(1, nx):
                o = other(x, q, nx)
                arrived(piece(k, zi, o), sx.at[k, zi, q], rx.at[k, zi, o])

    def finish(k):
        @pl.when(jnp.logical_not(crossed(k)))
        def _():
            for q in range(1, np_):
                first_a(k, q).wait_send()
            for q in range(1, nx):
                second_a(k, q).wait_send()

        @pl.when(crossed(k))
        def _():
            for q in range(1, nx):
                first_b(k, q).wait_send()
            for q in range(1, np_):
                second_b(k, q).wait_send()

        for q in range(1, nz):
            along_z(k, q).wait_send()
            gather_z(k, q).wait_send()
        for zo in range(nz):
            for q in range(1, nx):
                gather_x(k, zo, q).wait_send()

    barrier = pltpu.get_barrier_semaphore()
    peers = [to_pair(q) for q in range(1, np_)] + [to_x(q) for q in range(1, nx)] + [to_z(q) for q in range(1, nz)]
    for peer in peers:
        pl.semaphore_signal(barrier, inc=1, device_id=peer, device_id_type=pl.DeviceIdType.MESH)

    loads = [pltpu.make_async_copy(act_hbm, act_ref, load.at[0]), pltpu.make_async_copy(cot_hbm, cot_ref, load.at[1])]
    for copy in loads:
        copy.start()
    loads[0].wait()
    act_t[...] = act_ref[...].T
    loads[1].wait()
    width = 2 if nc % 2 == 0 else 1

    def compute(g):
        for xi in range(nx):
            col = pl.multiple_of(xi * cols_x + g * (width * LANES), LANES)
            grad = jnp.dot(act_t[...], cot_ref[:, pl.ds(col, width * LANES)], preferred_element_type=jnp.float32)
            for w in range(width):
                for pi in range(np_):
                    for zi in range(nz):
                        for s in range(ns):
                            row = pi * rows_p + (zi * ns + s) * rs
                            part[(g * width + w) * ns + s, pi, xi, zi] = grad[row:row + rs, w * LANES:(w + 1) * LANES]

    groups = nc // width
    early = max(1, groups // 2)
    pl.loop(0, early)(compute)
    pl.semaphore_wait(barrier, len(peers))
    ahead = min(AHEAD, early * width * ns)
    for k in range(ahead):
        start_first(k)
    pl.loop(early, groups)(compute)

    @pl.loop(0, chunks + LAG[2])
    def _(t):
        pl.when(t + ahead < chunks)(lambda: start_first(t + ahead))
        pl.when(t < chunks)(lambda: stage2(t))
        pl.when((t >= LAG[0]) & (t - LAG[0] < chunks))(lambda: stage3(t - LAG[0]))
        pl.when((t >= LAG[1]) & (t - LAG[1] < chunks))(lambda: stage4(t - LAG[1]))
        pl.when(t >= LAG[2])(lambda: stage5(t - LAG[2]))

    @pl.loop(0, chunks)
    def _(k):
        stage6(k)
        finish(k)


def solution(mesh):
    np_, ndp = mesh.shape["pair"], mesh.shape["dp"]
    nx = 1
    while (2 * nx) ** 2 <= ndp and ndp % (2 * nx) == 0:
        nx *= 2
    nz = ndp // nx

    def local(activations, cotangents):
        rows, cols = activations.shape[1], cotangents.shape[1]
        nc = cols // nx // LANES
        ns = SPLIT
        rs = rows // np_ // nz // ns
        chunks = nc * ns
        wide = max(np_, nx)
        f32 = jnp.float32
        dma = pltpu.SemaphoreType.DMA
        return pl.pallas_call(
            functools.partial(kernel, np_, nx, nz, nc, ns),
            out_shape=jax.ShapeDtypeStruct((rows // np_, cols), jnp.bfloat16),
            in_specs=[pl.BlockSpec(memory_space=pltpu.HBM)] * 2,
            out_specs=pl.BlockSpec(memory_space=pltpu.VMEM),
            scratch_shapes=[
                pltpu.VMEM(activations.shape, activations.dtype),
                pltpu.VMEM(cotangents.shape, cotangents.dtype),
                pltpu.VMEM((rows, activations.shape[0]), activations.dtype),
                pltpu.VMEM((chunks, np_, nx, nz, rs, LANES), f32),
                pltpu.VMEM((chunks, np_ * nx, nz, rs, LANES), f32),
                pltpu.VMEM((chunks, wide, nz, rs, LANES), f32),
                pltpu.VMEM((chunks, nz, rs, LANES), f32),
                dma((chunks, wide)), dma((chunks, wide)),
                dma((chunks, wide)), dma((chunks, wide)),
                dma((chunks, nz)), dma((chunks, nz)),
                dma((chunks, nz)), dma((chunks, nz)),
                dma((chunks, nz, nx)), dma((chunks, nz, nx)),
                dma((2,)),
            ],
            compiler_params=pltpu.CompilerParams(
                collective_id=0, has_side_effects=True, vmem_limit_bytes=60 * 1024 * 1024),
        )(activations, cotangents)

    in_specs = (P(("pair", "dp"), "ep"), P(("pair", "dp"), "ep"))
    return jax.shard_map(local, mesh=mesh, in_specs=in_specs, out_specs=P("pair", "ep"), check_vma=False)
```

profile of v0, /device:TPU:0, one launch (start us, length us, event | category | flops | bytes accessed | tf_op | source)
XLA Modules:
  0.0 68.4 jit_solution(11904001508774295478)
XLA Ops:
  0.0 66.1 %shard_map.28 = bf16[256,2048]{1,0:T(8,128)(2,1)} custom-call(bf16[768,512]{1,0:T(8,128)(2,1)} %act_hbm.1, bf16[768,2048]{1,0:T(8,128)(2,1)} %cot_hbm.1), custom_call_target="tpu_custom_call" | custom-call | tf_op jit(solution)/shard_map/pallas_call | solution.py:243
  66.1 2.3 %copy.4 = bf16[256,2048]{1,0:T(8,128)(2,1)} copy(bf16[256,2048]{1,0:T(8,128)(2,1)} %shard_map.28) | data formatting | bytes 2097152
where the time goes:
time: 68.5 us; the launch traced here: 68.4 us
  Pallas kernels  66.1 us (96%)
  local copies, waits for them, and re-layouts  2.3 us (3%)
    pallas_call x1, Pallas kernels, local(): pl.pallas_call(functools.partial(kernel, np_, nx, nz, nc, ns), out_shape=...  66.1 us
    unnamed x1, local copies, waits for them, and re-layouts  2.3 us

commit v1 on v0

--- a/solution.py
+++ b/solution.py
@@ -1,4 +1,5 @@
 import functools
+import math
 
 import jax
 import jax.numpy as jnp
@@ -12,9 +13,31 @@
 AHEAD = 3
 CROSS = 2
 LAG = (4, 7, 10)
-
-
-def kernel(np_, nx, nz, nc, ns, act_hbm, cot_hbm, out_ref, act_ref, cot_ref, act_t, part, f1, f2, zr,
+POWER = 11
+LARGEST_PRODUCT = 16 * 1.75
+
+
+def scale_and_offset(terms):
+    scale = 2.0 ** math.floor(126 / POWER - math.log2(terms * LARGEST_PRODUCT))
+    return scale, 2.0 ** (-124 / POWER)
+
+
+def encode(x, terms):
+    scale, offset = scale_and_offset(terms)
+    a = x * scale + jnp.where(x < 0, -offset, offset)
+    a2 = a * a
+    a4 = a2 * a2
+    return (a4 * a4 * (a2 * a)).astype(jnp.bfloat16)
+
+
+def decode(f, terms):
+    scale, offset = scale_and_offset(terms)
+    f = f.astype(jnp.float32)
+    a = (jnp.exp2(jnp.log2(jnp.abs(f)) * (1 / POWER)) - offset) * (1 / scale)
+    return jnp.where(f < 0, -a, a)
+
+
+def kernel(np_, nx, nz, nc, ns, act_hbm, cot_hbm, out_ref, act_ref, cot_ref, act_t, part, enc, f1, f2, zr,
            s1, r1, s2, r2, sz, rz, sg, rg, sx, rx, load):
     p = lax.axis_index("pair")
     dp = lax.axis_index("dp")
@@ -23,6 +46,7 @@
     chunks = nc * ns
     rows_p = nz * ns * rs
     cols_x = nc * LANES
+    terms = act_ref.shape[0]
 
     def other(i, q, n):
         return lax.rem(i + q, n)
@@ -45,21 +69,21 @@
             device_id=peer, device_id_type=pl.DeviceIdType.MESH)
 
     def first_a(k, q):
-        return remote(part.at[k, other(p, q, np_)], f1.at[k, pl.ds(p * nx, nx)],
+        return remote(enc.at[k, other(p, q, np_)], f1.at[k, pl.ds(p * nx, nx)],
                       s1.at[k, q], r1.at[k, p], to_pair(q))
 
     def first_b(k, q):
-        return remote(part.at[k, :, other(x, q, nx)], f1.at[k, pl.ds(x * np_, np_)],
+        return remote(enc.at[k, :, other(x, q, nx)], f1.at[k, pl.ds(x * np_, np_)],
                       s1.at[k, q], r1.at[k, x], to_x(q))
 
     def second_a(k, q):
-        return remote(part.at[k, p, other(x, q, nx)], f2.at[k, x], s2.at[k, q], r2.at[k, x], to_x(q))
+        return remote(enc.at[k, p, other(x, q, nx)], f2.at[k, x], s2.at[k, q], r2.at[k, x], to_x(q))
 
     def second_b(k, q):
-        return remote(part.at[k, other(p, q, np_), x], f2.at[k, p], s2.at[k, q], r2.at[k, p], to_pair(q))
+        return remote(enc.at[k, other(p, q, np_), x], f2.at[k, p], s2.at[k, q], r2.at[k, p], to_pair(q))
 
     def along_z(k, q):
-        return remote(part.at[k, p, x, other(z, q, nz)], zr.at[k, z], sz.at[k, q], rz.at[k, z], to_z(q))
+        return remote(enc.at[k, p, x, other(z, q, nz)], zr.at[k, z], sz.at[k, q], rz.at[k, z], to_z(q))
 
     def piece(k, zi, xi):
         c, s = k // ns, lax.rem(k, ns)
@@ -83,11 +107,15 @@
         @pl.when(crossed(k))
         def _():
             for q in range(1, nx):
+                o = other(x, q, nx)
+                enc[k, :, o] = encode(part[k, :, o], terms)
                 first_b(k, q).start()
 
         @pl.when(jnp.logical_not(crossed(k)))
         def _():
             for q in range(1, np_):
+                o = other(p, q, np_)
+                enc[k, o] = encode(part[k, o], terms)
                 first_a(k, q).start()
 
     def stage2(k):
@@ -97,8 +125,10 @@
                 o = other(p, q, np_)
                 arrived(f1.at[k, pl.ds(o * nx, nx)], s1.at[k, q], r1.at[k, o])
                 for i in range(nx):
-                    part[k, p, i] += f1[k, o * nx + i]
-            for q in range(1, nx):
+                    part[k, p, i] += decode(f1[k, o * nx + i], terms)
+            for q in range(1, nx):
+                o = other(x, q, nx)
+                enc[k, p, o] = encode(part[k, p, o], np_ * terms)
                 second_a(k, q).start()
 
         @pl.when(crossed(k))
@@ -107,8 +137,10 @@
                 o = other(x, q, nx)
                 arrived(f1.at[k, pl.ds(o * np_, np_)], s1.at[k, q], r1.at[k, o])
                 for i in range(np_):
-                    part[k, i, x] += f1[k, o * np_ + i]
-            for q in range(1, np_):
+                    part[k, i, x] += decode(f1[k, o * np_ + i], terms)
+            for q in range(1, np_):
+                o = other(p, q, np_)
+                enc[k, o, x] = encode(part[k, o, x], nx * terms)
                 second_b(k, q).start()
 
     def stage3(k):
@@ -117,16 +149,18 @@
             for q in range(1, nx):
                 o = other(x, q, nx)
                 arrived(f2.at[k, o], s2.at[k, q], r2.at[k, o])
-                part[k, p, x] += f2[k, o]
+                part[k, p, x] += decode(f2[k, o], np_ * terms)
 
         @pl.when(crossed(k))
         def _():
             for q in range(1, np_):
                 o = other(p, q, np_)
                 arrived(f2.at[k, o], s2.at[k, q], r2.at[k, o])
-                part[k, p, x] += f2[k, o]
+                part[k, p, x] += decode(f2[k, o], nx * terms)
 
         for q in range(1, nz):
+            o = other(z, q, nz)
+            enc[k, p, x, o] = encode(part[k, p, x, o], np_ * nx * terms)
             along_z(k, q).start()
 
     def stage4(k):
@@ -134,7 +168,7 @@
         for q in range(1, nz):
             o = other(z, q, nz)
             arrived(zr.at[k, o], sz.at[k, q], rz.at[k, o])
-            total = total + zr[k, o]
+            total = total + decode(zr[k, o], np_ * nx * terms)
         replicas = np_ * nx * nz
         piece(k, z, x)[...] = (total / replicas).astype(out_ref.dtype)
         for q in range(1, nz):
@@ -238,7 +272,7 @@
         rs = rows // np_ // nz // ns
         chunks = nc * ns
         wide = max(np_, nx)
-        f32 = jnp.float32
+        f32, bf16 = jnp.float32, jnp.bfloat16
         dma = pltpu.SemaphoreType.DMA
         return pl.pallas_call(
             functools.partial(kernel, np_, nx, nz, nc, ns),
@@ -250,9 +284,10 @@
                 pltpu.VMEM(cotangents.shape, cotangents.dtype),
                 pltpu.VMEM((rows, activations.shape[0]), activations.dtype),
                 pltpu.VMEM((chunks, np_, nx, nz, rs, LANES), f32),
-                pltpu.VMEM((chunks, np_ * nx, nz, rs, LANES), f32),
-                pltpu.VMEM((chunks, wide, nz, rs, LANES), f32),
-                pltpu.VMEM((chunks, nz, rs, LANES), f32),
+                pltpu.VMEM((chunks, np_, nx, nz, rs, LANES), bf16),
+                pltpu.VMEM((chunks, np_ * nx, nz, rs, LANES), bf16),
+                pltpu.VMEM((chunks, wide, nz, rs, LANES), bf16),
+                pltpu.VMEM((chunks, nz, rs, LANES), bf16),
                 dma((chunks, wide)), dma((chunks, wide)),
                 dma((chunks, wide)), dma((chunks, wide)),
                 dma((chunks, nz)), dma((chunks, nz)),

time: 68.5 us -> 53.2 us (0.78)
  Pallas kernels: 66.1 us -> 50.7 us
    pallas_call x1, Pallas kernels: 66.1 us -> 50.7 us  [local(): pl.pallas_call(functools.partial(kernel, np_, nx, nz, nc, ns), out_shape=...]
where the time goes in v1:
time: 53.2 us; the launch traced here: 53 us
  Pallas kernels  50.7 us (95%)
  local copies, waits for them, and re-layouts  2.3 us (4%)
    pallas_call x1, Pallas kernels, local(): pl.pallas_call(functools.partial(kernel, np_, nx, nz, nc, ns), out_shape=...  50.7 us
    unnamed x1, local copies, waits for them, and re-layouts  2.3 us

profile of v1, /device:TPU:0, one launch (start us, length us, event | category | flops | bytes accessed | tf_op | source)
XLA Modules:
  0.0 53.0 jit_solution(10753055444691305569)
XLA Ops:
  0.0 50.7 %shard_map.28 = bf16[256,2048]{1,0:T(8,128)(2,1)} custom-call(bf16[768,512]{1,0:T(8,128)(2,1)} %act_hbm.1, bf16[768,2048]{1,0:T(8,128)(2,1)} %cot_hbm.1), custom_call_target="tpu_custom_call" | custom-call | tf_op jit(solution)/shard_map/pallas_call | solution.py:277
  50.7 2.3 %copy.4 = bf16[256,2048]{1,0:T(8,128)(2,1)} copy(bf16[256,2048]{1,0:T(8,128)(2,1)} %shard_map.28) | data formatting | bytes 2097152

commit v2 on v1

v2 whole, which is shorter than its diff:
```python
import functools
import math

import jax
import jax.numpy as jnp
from jax import lax
from jax.experimental import pallas as pl
from jax.experimental.pallas import tpu as pltpu
from jax.sharding import PartitionSpec as P

LANES = 128
SPLIT = 2
POWER = 11
LARGEST_PRODUCT = 16 * 1.75
VM = 20
Y_FIRST = "AB"
X_GATHER = "0"
AHEAD = 8
LAGS = (0, 3, 7, 11, 12, 15)


def scale_and_offset(terms):
    scale = 2.0 ** math.floor(126 / POWER - math.log2(terms * LARGEST_PRODUCT))
    return scale, 2.0 ** (-124 / POWER)


def encode(x, terms):
    scale, offset = scale_and_offset(terms)
    a = x * scale + jnp.where(x < 0, -offset, offset)
    a2 = a * a
    a4 = a2 * a2
    return (a4 * a4 * (a2 * a)).astype(jnp.bfloat16)


def decode(f, terms):
    scale, offset = scale_and_offset(terms)
    f = f.astype(jnp.float32)
    a = jnp.exp2(jnp.log2(jnp.abs(f)) * (1 / POWER) - math.log2(scale)) - offset / scale
    return jnp.where(f < 0, -a, a)


def kernel(np_, nx, nz, nc, ns, act_hbm, cot_hbm, out_ref, act_ref, cot_ref, act_t, part, enc, f1, f2, zr,
           s1, r1, s2, r2, sz, rz, sgz, sgx, sr, rn, rf, rl, load):
    p = lax.axis_index("pair")
    dp = lax.axis_index("dp")
    z, x = dp // nx, dp % nx
    rs = part.shape[-2]
    chunks = nc * ns
    rows_p = nz * ns * rs
    cols_x = nc * LANES
    terms = act_ref.shape[0]
    replicas = np_ * nx * nz
    half = max(1, nz // 2)
    low = z < half
    base = jnp.where(low, 0, half)
    far = jnp.where(low, half, 0)
    gateway = jnp.where(low, half - 1, half)
    opposite = jnp.where(low, half, half - 1)

    def other(i, q, n):
        return lax.rem(i + q, n)

    def to_pair(q):
        return {"pair": other(p, q, np_)}

    def to_x(q):
        return {"dp": z * nx + other(x, q, nx)}

    def at_z(zi):
        return {"dp": zi * nx + x}

    def near(q):
        return base + other(z - base, q, half)

    def y_first(k):
        return Y_FIRST[k % len(Y_FIRST)] == "A"

    def x_gather(k):
        return int(X_GATHER[k % len(X_GATHER)])

    def remote(src, dst, ssem, rsem, peer):
        return pltpu.make_async_remote_copy(
            src_ref=src, dst_ref=dst, send_sem=ssem, recv_sem=rsem,
            device_id=peer, device_id_type=pl.DeviceIdType.MESH)

    def arrived(ref, rsem):
        remote(ref, ref, rsem, rsem, to_pair(1)).wait_recv()

    def sent(ref, ssem):
        remote(ref, ref, ssem, ssem, to_pair(1)).wait_send()

    def piece(k, zi, xi):
        c, s = k // ns, k % ns
        row = pl.multiple_of((zi * ns + s) * rs, rs)
        col = pl.multiple_of(xi * cols_x + c * LANES, LANES)
        return out_ref.at[pl.ds(row, rs), pl.ds(col, LANES)]

    def spread(k, zi, xi, peer, ssem, rsem):
        here = piece(k, zi, xi)
        remote(here, here, ssem, rsem, peer).start()

    def gather_z(k, xi):
        t = x_gather(k)
        if nz > 1:
            spread(k, z, xi, at_z(opposite), sgz.at[t], rf.at[k])
        for q in range(1, half):
            spread(k, z, xi, at_z(near(q)), sgz.at[t], rl.at[1] if t else rn.at[k])

    def gather_x(k, zi):
        t = x_gather(k)
        for q in range(1, nx):
            spread(k, zi, x, to_x(q), sgx.at[t], rn.at[k] if t else rl.at[0])

    def stage_first(k):
        if y_first(k):
            for q in range(1, np_):
                o = other(p, q, np_)
                enc[k, o] = encode(part[k, o], terms)
                remote(enc.at[k, o], f1.at[k, pl.ds(p * nx, nx)], s1.at[0], r1.at[k], to_pair(q)).start()
        else:
            for q in range(1, nx):
                o = other(x, q, nx)
                enc[k, :, o] = encode(part[k, :, o], terms)
                remote(enc.at[k, :, o], f1.at[k, pl.ds(x * np_, np_)], s1.at[1], r1.at[k], to_x(q)).start()

    def stage_second(k):
        if y_first(k):
            arrived(f1.at[k, pl.ds(0, (np_ - 1) * nx)], r1.at[k])
            for q in range(1, np_):
                o = other(p, q, np_)
                part[k, p] += decode(f1[k, pl.ds(o * nx, nx)], terms)
            for q in range(1, nx):
                o = other(x, q, nx)
                enc[k, p, o] = encode(part[k, p, o], np_ * terms)
                remote(enc.at[k, p, o], f2.at[k, x], s2.at[0], r2.at[k], to_x(q)).start()
        else:
            arrived(f1.at[k, pl.ds(0, (nx - 1) * np_)], r1.at[k])
            for q in range(1, nx):
                o = other(x, q, nx)
                part[k, :, x] += decode(f1[k, pl.ds(o * np_, np_)], terms)
            for q in range(1, np_):
                o = other(p, q, np_)
                enc[k, o, x] = encode(part[k, o, x], nx * terms)
                remote(enc.at[k, o, x], f2.at[k, p], s2.at[1], r2.at[k], to_pair(q)).start()

    def stage_third(k):
        n, i, count = (nx, x, np_) if y_first(k) else (np_, p, nx)
        arrived(f2.at[k, pl.ds(0, n - 1)], r2.at[k])
        for q in range(1, n):
            part[k, p, x] += decode(f2[k, other(i, q, n)], count * terms)
        for q in range(1, nz):
            o = other(z, q, nz)
            enc[k, p, x, o] = encode(part[k, p, x, o], np_ * nx * terms)
            remote(enc.at[k, p, x, o], zr.at[k, z], sz, rz.at[k], at_z(o)).start()

    def stage_own(k):
        total = part[k, p, x, z]
        if nz > 1:
            arrived(zr.at[k, pl.ds(0, nz - 1)], rz.at[k])
        for q in range(1, nz):
            total = total + decode(zr[k, other(z, q, nz)], np_ * nx * terms)
        piece(k, z, x)[...] = (total / replicas).astype(out_ref.dtype)
        if x_gather(k):
            gather_x(k, z)
            gather_z(k, x)
        else:
            gather_z(k, x)
            gather_x(k, z)

    def stage_near(k):
        if x_gather(k):
            arrived(enc.at[k, 0, pl.ds(0, nx - 1), 0], rn.at[k])
            for q in range(1, nx):
                gather_z(k, other(x, q, nx))
        elif half > 1:
            arrived(enc.at[k, 0, 0, pl.ds(0, half - 1)], rn.at[k])
            for q in range(1, half):
                gather_x(k, near(q))

    def far_bytes(k):
        return enc.at[k, 0, :, pl.ds(0, half)] if x_gather(k) else enc.at[k, 0, 0, pl.ds(0, half)]

    def stage_relay(k):
        t = x_gather(k)
        if half > 1:
            @pl.when(z == gateway)
            def _():
                arrived(far_bytes(k), rf.at[k])
                for j in range(half):
                    for xi in [x] + [other(x, q, nx) for q in range(1, nx if t else 1)]:
                        for q in range(1, half):
                            spread(k, far + j, xi, at_z(near(q)), sr.at[t, q], rf.at[k])

    def stage_far(k):
        if half > 1:
            @pl.when(z != gateway)
            def _():
                arrived(far_bytes(k), rf.at[k])
        elif nz > 1:
            arrived(far_bytes(k), rf.at[k])
        if nz > 1 and not x_gather(k):
            for j in range(half):
                gather_x(k, far + j)

    def drain():
        kinds = [sum(1 for k in range(chunks) if not y_first(k)), sum(1 for k in range(chunks) if x_gather(k))]
        a, b = chunks - kinds[0], kinds[0]
        g0, g1 = chunks - kinds[1], kinds[1]
        if a:
            sent(enc.at[pl.ds(0, a), pl.ds(0, np_ - 1)], s1.at[0])
            sent(enc.at[pl.ds(0, a), 0, pl.ds(0, nx - 1)], s2.at[0])
        if b:
            sent(enc.at[pl.ds(0, b), :, pl.ds(0, nx - 1)], s1.at[1])
            sent(enc.at[pl.ds(0, b), pl.ds(0, np_ - 1), 0], s2.at[1])
        if nz > 1:
            sent(enc.at[:, 0, 0, pl.ds(0, nz - 1)], sz)
        for t, g in ((0, g0), (1, g1)):
            if not g:
                continue
            if nz > 1:
                wide = enc.at[pl.ds(0, g), 0, :, pl.ds(0, half)] if t else enc.at[pl.ds(0, g), 0, 0, pl.ds(0, half)]
                sent(wide, sgz.at[t])
                if half > 1:
                    @pl.when(z == gateway)
                    def _():
                        for q in range(1, half):
                            sent(wide, sr.at[t, q])
            if t:
                sent(enc.at[pl.ds(0, g), 0, pl.ds(0, nx - 1), 0], sgx.at[t])
                if half > 1:
                    arrived(enc.at[pl.ds(0, g), 0, :, pl.ds(0, half - 1)], rl.at[t])
            else:
                sent(enc.at[pl.ds(0, g), 0, pl.ds(0, nx - 1)], sgx.at[t])
                arrived(enc.at[pl.ds(0, g), 0, pl.ds(0, nx - 1)], rl.at[t])

    barrier = pltpu.get_barrier_semaphore()
    peers = [to_pair(q) for q in range(1, np_)] + [to_x(q) for q in range(1, nx)] + [at_z(other(z, q, nz)) for q in range(1, nz)]
    for peer in peers:
        pl.semaphore_signal(barrier, inc=1, device_id=peer, device_id_type=pl.DeviceIdType.MESH)

    width = 2 if nc % 2 == 0 else 1
    groups = nc // width
    blocks = [(g, xi) for g in range(groups) for xi in range(nx)]

    def block(g, xi):
        return pl.ds(xi * cols_x + g * (width * LANES), width * LANES)

    loads = [pltpu.make_async_copy(act_hbm, act_ref, load.at[len(blocks)])]
    loads += [pltpu.make_async_copy(cot_hbm.at[:, block(g, xi)], cot_ref.at[:, block(g, xi)], load.at[i])
              for i, (g, xi) in enumerate(blocks)]
    for copy in loads:
        copy.start()
    loads[0].wait()
    act_t[...] = act_ref[...].T

    def compute(g):
        for xi in range(nx):
            loads[1 + g * nx + xi].wait()
            grad = jnp.dot(act_t[...], cot_ref[:, block(g, xi)], preferred_element_type=jnp.float32)
            for w in range(width):
                for pi in range(np_):
                    for zi in range(nz):
                        for s in range(ns):
                            row = pi * rows_p + (zi * ns + s) * rs
                            part[(g * width + w) * ns + s, pi, xi, zi] = grad[row:row + rs, w * LANES:(w + 1) * LANES]

    per = width * ns
    stages = [stage_first, stage_second, stage_third, stage_own, stage_near, stage_relay, stage_far]
    lags = (-AHEAD,) + LAGS
    events = sorted((k + lags[i], -i, k) for k in range(chunks) for i in range(len(stages)))
    done = 0
    waited = False
    for _, i, k in events:
        while done <= k // per:
            compute(done)
            done += 1
        if not waited:
            pl.semaphore_wait(barrier, len(peers))
            waited = True
        stages[-i](k)
    drain()


def solution(mesh):
    np_, ndp = mesh.shape["pair"], mesh.shape["dp"]
    nx = 1
    while (2 * nx) ** 2 <= ndp and ndp % (2 * nx) == 0:
        nx *= 2
    nz = ndp // nx

    def local(activations, cotangents):
        rows, cols = activations.shape[1], cotangents.shape[1]
        nc = cols // nx // LANES
        ns = SPLIT
        rs = rows // np_ // nz // ns
        chunks = nc * ns
        wide = max(np_, nx)
        f32, bf16 = jnp.float32, jnp.bfloat16
        dma = pltpu.SemaphoreType.DMA
        activations, cotangents = (pltpu.with_memory_space_constraint(a, pltpu.HBM) for a in (activations, cotangents))
        return pl.pallas_call(
            functools.partial(kernel, np_, nx, nz, nc, ns),
            out_shape=jax.ShapeDtypeStruct((rows // np_, cols), jnp.bfloat16),
            in_specs=[pl.BlockSpec(memory_space=pltpu.HBM)] * 2,
            out_specs=pl.BlockSpec(memory_space=pltpu.VMEM),
            scratch_shapes=[
                pltpu.VMEM(activations.shape, activations.dtype),
                pltpu.VMEM(cotangents.shape, cotangents.dtype),
                pltpu.VMEM((rows, activations.shape[0]), activations.dtype),
                pltpu.VMEM((chunks, np_, nx, nz, rs, LANES), f32),
                pltpu.VMEM((chunks, np_, nx, nz, rs, LANES), bf16),
                pltpu.VMEM((chunks, np_ * nx, nz, rs, LANES), bf16),
                pltpu.VMEM((chunks, wide, nz, rs, LANES), bf16),
                pltpu.VMEM((chunks, nz, rs, LANES), bf16),
                dma((2,)), dma((chunks,)), dma((2,)), dma((chunks,)), dma(()), dma((chunks,)),
                dma((2,)), dma((2,)), dma((2, nz)), dma((chunks,)), dma((chunks,)), dma((2,)),
                dma((1 + nc * nx,)),
            ],
            compiler_params=pltpu.CompilerParams(
                collective_id=0, has_side_effects=True, vmem_limit_bytes=VM * 1024 * 1024),
        )(activations, cotangents)

    in_specs = (P(("pair", "dp"), "ep"), P(("pair", "dp"), "ep"))
    return jax.shard_map(local, mesh=mesh, in_specs=in_specs, out_specs=P("pair", "ep"), check_vma=False)
```

time: 53.2 us -> 46.4 us (0.87)
  Pallas kernels: 50.7 us -> 45.3 us
  local copies, waits for them, and re-layouts: 2.3 us -> 0.97 us
    pallas_call x1, Pallas kernels: 50.7 us -> 45.3 us  [local(): pl.pallas_call(functools.partial(kernel, np_, nx, nz, nc, ns), out_shape=...]
    unnamed x1, local copies, waits for them, and re-layouts: 2.3 us -> 0.97 us
where the time goes in v2:
time: 46.4 us; the launch traced here: 46.3 us
  Pallas kernels  45.3 us (98%)
  local copies, waits for them, and re-layouts  0.97 us (2%)
    pallas_call x1, Pallas kernels, local(): pl.pallas_call(functools.partial(kernel, np_, nx, nz, nc, ns), out_shape=...  45.3 us
    unnamed x1, local copies, waits for them, and re-layouts  0.97 us

profile of v2, /device:TPU:0, one launch (start us, length us, event | category | flops | bytes accessed | tf_op | source)
XLA Modules:
  0.0 46.3 jit_solution(16819187541063546968)
XLA Ops:
  0.0 45.3 %shard_map.28 = bf16[256,2048]{1,0:T(8,128)(2,1)S(1)} custom-call(bf16[768,512]{1,0:T(8,128)(2,1)} %act_hbm.1, bf16[768,2048]{1,0:T(8,128)(2,1)} %cot_hbm.1), custom_call_target="tpu_custom_call" | custom-call | tf_op jit(solution)/shard_map/pallas_call | solution.py:301
  45.3 1.0 %copy.4 = bf16[256,2048]{1,0:T(8,128)(2,1)} copy(bf16[256,2048]{1,0:T(8,128)(2,1)S(1)} %shard_map.28) | data formatting | bytes 2097152

commit v3 on v2

--- a/solution.py
+++ b/solution.py
@@ -13,10 +13,17 @@
 POWER = 11
 LARGEST_PRODUCT = 16 * 1.75
 VM = 20
-Y_FIRST = "AB"
+KINDS = "CCCABABABABABABA"
+CSLOTS = (-9, 6, 11, 15, 19, 20, 24, 2)
+CSTEP = 2
+RATE = 1
+SA = 2
+SB = 2
+OB = 1
 X_GATHER = "0"
-AHEAD = 8
-LAGS = (0, 3, 7, 11, 12, 15)
+AHEAD = 4
+LAGS = (0, 4, 9, 14, 15, 19)
+XLAGS = (12, 17, 21)
 
 
 def scale_and_offset(terms):
@@ -39,8 +46,8 @@
     return jnp.where(f < 0, -a, a)
 
 
-def kernel(np_, nx, nz, nc, ns, act_hbm, cot_hbm, out_ref, act_ref, cot_ref, act_t, part, enc, f1, f2, zr,
-           s1, r1, s2, r2, sz, rz, sgz, sgx, sr, rn, rf, rl, load):
+def kernel(np_, nx, nz, nc, ns, act_hbm, cot_hbm, out_ref, act_ref, cot_ref, act_t, part, enc, f1, f2, zr, fc, fg, fy, fx,
+           s1, r1, rg, s2, r2, sz, rz, sgz, sgx, sr, rn, rf, rl, load):
     p = lax.axis_index("pair")
     dp = lax.axis_index("dp")
     z, x = dp // nx, dp % nx
@@ -72,8 +79,8 @@
     def near(q):
         return base + other(z - base, q, half)
 
-    def y_first(k):
-        return Y_FIRST[k % len(Y_FIRST)] == "A"
+    def kind(k):
+        return KINDS[k % len(KINDS)]
 
     def x_gather(k):
         return int(X_GATHER[k % len(X_GATHER)])
@@ -111,8 +118,22 @@
         for q in range(1, nx):
             spread(k, zi, x, to_x(q), sgx.at[t], rn.at[k] if t else rl.at[0])
 
+    cs = [k for k in range(chunks) if kind(k) == "C"]
+
     def stage_first(k):
-        if y_first(k):
+        if kind(k) == "C":
+            c = cs.index(k)
+            if half > 1:
+                @pl.when(z != gateway)
+                def _():
+                    for j in range(half):
+                        enc[k, :, :, far + j] = encode(part[k, :, :, far + j], terms)
+                        remote(enc.at[k, :, :, far + j], fg.at[c, z - base, j], s1.at[3], rg.at[c], at_z(gateway)).start()
+            for q in range(1, half):
+                o = near(q)
+                enc[k, :, :, o] = encode(part[k, :, :, o], terms)
+                remote(enc.at[k, :, :, o], fc.at[c, z], s1.at[2], r1.at[k], at_z(o)).start()
+        elif kind(k) == "A":
             for q in range(1, np_):
                 o = other(p, q, np_)
                 enc[k, o] = encode(part[k, o], terms)
@@ -123,8 +144,32 @@
                 enc[k, :, o] = encode(part[k, :, o], terms)
                 remote(enc.at[k, :, o], f1.at[k, pl.ds(x * np_, np_)], s1.at[1], r1.at[k], to_x(q)).start()
 
+    def stage_pre(k):
+        c = cs.index(k)
+
+        @pl.when(z == gateway)
+        def _():
+            if half > 1:
+                arrived(fg.at[c, pl.ds(0, half - 1)], rg.at[c])
+            for j in range(half):
+                total = part[k, :, :, far + j]
+                for q in range(1, half):
+                    total = total + decode(fg[c, near(q) - base, j], terms)
+                enc[k, :, :, far + j] = encode(total, half * terms)
+                remote(enc.at[k, :, :, far + j], fc.at[c, base], s1.at[3], r1.at[k], at_z(far + j)).start()
+
     def stage_second(k):
-        if y_first(k):
+        if kind(k) == "C":
+            c = cs.index(k)
+            arrived(fc.at[c, pl.ds(0, half)], r1.at[k])
+            part[k, :, :, z] += decode(fc[c, far], half * terms)
+            for q in range(1, half):
+                part[k, :, :, z] += decode(fc[c, near(q)], terms)
+            for q in range(1, np_):
+                o = other(p, q, np_)
+                enc[k, o, :, z] = encode(part[k, o, :, z], nz * terms)
+                remote(enc.at[k, o, :, z], fy.at[cs.index(k), p], s2.at[2], r2.at[k], to_pair(q)).start()
+        elif kind(k) == "A":
             arrived(f1.at[k, pl.ds(0, (np_ - 1) * nx)], r1.at[k])
             for q in range(1, np_):
                 o = other(p, q, np_)
@@ -144,20 +189,33 @@
                 remote(enc.at[k, o, x], f2.at[k, p], s2.at[1], r2.at[k], to_pair(q)).start()
 
     def stage_third(k):
-        n, i, count = (nx, x, np_) if y_first(k) else (np_, p, nx)
+        if kind(k) == "C":
+            arrived(fy.at[cs.index(k), pl.ds(0, np_ - 1)], r2.at[k])
+            for q in range(1, np_):
+                part[k, p, :, z] += decode(fy[cs.index(k), other(p, q, np_)], nz * terms)
+            for q in range(1, nx):
+                o = other(x, q, nx)
+                enc[k, p, o, z] = encode(part[k, p, o, z], np_ * nz * terms)
+                remote(enc.at[k, p, o, z], fx.at[cs.index(k), x], sz.at[1], rz.at[k], to_x(q)).start()
+            return
+        n, i, count = (nx, x, np_) if kind(k) == "A" else (np_, p, nx)
         arrived(f2.at[k, pl.ds(0, n - 1)], r2.at[k])
         for q in range(1, n):
             part[k, p, x] += decode(f2[k, other(i, q, n)], count * terms)
         for q in range(1, nz):
             o = other(z, q, nz)
             enc[k, p, x, o] = encode(part[k, p, x, o], np_ * nx * terms)
-            remote(enc.at[k, p, x, o], zr.at[k, z], sz, rz.at[k], at_z(o)).start()
+            remote(enc.at[k, p, x, o], zr.at[k, z], sz.at[0], rz.at[k], at_z(o)).start()
 
     def stage_own(k):
         total = part[k, p, x, z]
-        if nz > 1:
+        if kind(k) == "C":
+            arrived(fx.at[cs.index(k), pl.ds(0, nx - 1)], rz.at[k])
+            for q in range(1, nx):
+                total = total + decode(fx[cs.index(k), other(x, q, nx)], np_ * nz * terms)
+        elif nz > 1:
             arrived(zr.at[k, pl.ds(0, nz - 1)], rz.at[k])
-        for q in range(1, nz):
+        for q in range(1, nz if kind(k) != "C" else 1):
             total = total + decode(zr[k, other(z, q, nz)], np_ * nx * terms)
         piece(k, z, x)[...] = (total / replicas).astype(out_ref.dtype)
         if x_gather(k):
@@ -203,17 +261,23 @@
                 gather_x(k, far + j)
 
     def drain():
-        kinds = [sum(1 for k in range(chunks) if not y_first(k)), sum(1 for k in range(chunks) if x_gather(k))]
-        a, b = chunks - kinds[0], kinds[0]
-        g0, g1 = chunks - kinds[1], kinds[1]
+        a, b, c = (sum(kind(k) == t for k in range(chunks)) for t in "ABC")
+        g1 = sum(x_gather(k) for k in range(chunks))
+        g0 = chunks - g1
         if a:
             sent(enc.at[pl.ds(0, a), pl.ds(0, np_ - 1)], s1.at[0])
             sent(enc.at[pl.ds(0, a), 0, pl.ds(0, nx - 1)], s2.at[0])
         if b:
             sent(enc.at[pl.ds(0, b), :, pl.ds(0, nx - 1)], s1.at[1])
             sent(enc.at[pl.ds(0, b), pl.ds(0, np_ - 1), 0], s2.at[1])
-        if nz > 1:
-            sent(enc.at[:, 0, 0, pl.ds(0, nz - 1)], sz)
+        if c:
+            if half > 1:
+                sent(enc.at[pl.ds(0, c), :, :, pl.ds(0, half - 1)], s1.at[2])
+            sent(enc.at[pl.ds(0, c), :, :, pl.ds(0, half)], s1.at[3])
+            sent(enc.at[pl.ds(0, c), pl.ds(0, np_ - 1), :, 0], s2.at[2])
+            sent(enc.at[pl.ds(0, c), 0, pl.ds(0, nx - 1), 0], sz.at[1])
+        if nz > 1 and a + b:
+            sent(enc.at[pl.ds(0, a + b), 0, 0, pl.ds(0, nz - 1)], sz.at[0])
         for t, g in ((0, g0), (1, g1)):
             if not g:
                 continue
@@ -245,8 +309,11 @@
     def block(g, xi):
         return pl.ds(xi * cols_x + g * (width * LANES), width * LANES)
 
+    def held(xi):
+        return pl.ds(xi * (width * LANES), width * LANES)
+
     loads = [pltpu.make_async_copy(act_hbm, act_ref, load.at[len(blocks)])]
-    loads += [pltpu.make_async_copy(cot_hbm.at[:, block(g, xi)], cot_ref.at[:, block(g, xi)], load.at[i])
+    loads += [pltpu.make_async_copy(cot_hbm.at[:, block(g, xi)], cot_ref.at[g, :, held(xi)], load.at[i])
               for i, (g, xi) in enumerate(blocks)]
     for copy in loads:
         copy.start()
@@ -256,22 +323,33 @@
     def compute(g):
         for xi in range(nx):
             loads[1 + g * nx + xi].wait()
-            grad = jnp.dot(act_t[...], cot_ref[:, block(g, xi)], preferred_element_type=jnp.float32)
+        grad = jnp.dot(act_t[...], cot_ref[g], preferred_element_type=jnp.float32)
+        for xi in range(nx):
             for w in range(width):
+                col = (xi * width + w) * LANES
                 for pi in range(np_):
                     for zi in range(nz):
                         for s in range(ns):
                             row = pi * rows_p + (zi * ns + s) * rs
-                            part[(g * width + w) * ns + s, pi, xi, zi] = grad[row:row + rs, w * LANES:(w + 1) * LANES]
+                            part[(g * width + w) * ns + s, pi, xi, zi] = grad[row:row + rs, col:col + LANES]
 
     per = width * ns
-    stages = [stage_first, stage_second, stage_third, stage_own, stage_near, stage_relay, stage_far]
-    lags = (-AHEAD,) + LAGS
-    events = sorted((k + lags[i], -i, k) for k in range(chunks) for i in range(len(stages)))
+    stages = [stage_first, stage_second, stage_third, stage_own, stage_near, stage_relay, stage_far, stage_pre]
+    lags = ((-AHEAD,) + LAGS, (-AHEAD,) + LAGS[:3] + XLAGS)
+    events = []
+    for k in range(chunks):
+        if kind(k) == "C":
+            j = cs.index(k)
+            slots = [CSLOTS[0]] + [slot + CSTEP * j for slot in CSLOTS[1:]]
+        else:
+            j = sum(kind(i) == kind(k) for i in range(k)) * (SA if kind(k) == "A" else SB) + (0 if kind(k) == "A" else OB)
+            slots = [RATE * j - AHEAD] + [j + lag for lag in lags[x_gather(k)][1:]]
+        events += [(slot, -i, k) for i, slot in enumerate(slots)]
+    events.sort()
     done = 0
     waited = False
     for _, i, k in events:
-        while done <= k // per:
+        while done < groups and (done <= k // per or -i not in (0, 7)):
             compute(done)
             done += 1
         if not waited:
@@ -292,9 +370,12 @@
         rows, cols = activations.shape[1], cotangents.shape[1]
         nc = cols // nx // LANES
         ns = SPLIT
+        width = 2 if nc % 2 == 0 else 1
         rs = rows // np_ // nz // ns
         chunks = nc * ns
         wide = max(np_, nx)
+        half = max(1, nz // 2)
+        cs = max(1, sum(KINDS[k % len(KINDS)] == "C" for k in range(chunks)))
         f32, bf16 = jnp.float32, jnp.bfloat16
         dma = pltpu.SemaphoreType.DMA
         activations, cotangents = (pltpu.with_memory_space_constraint(a, pltpu.HBM) for a in (activations, cotangents))
@@ -305,16 +386,20 @@
             out_specs=pl.BlockSpec(memory_space=pltpu.VMEM),
             scratch_shapes=[
                 pltpu.VMEM(activations.shape, activations.dtype),
-                pltpu.VMEM(cotangents.shape, cotangents.dtype),
+                pltpu.VMEM((nc // width, cotangents.shape[0], nx * width * LANES), cotangents.dtype),
                 pltpu.VMEM((rows, activations.shape[0]), activations.dtype),
                 pltpu.VMEM((chunks, np_, nx, nz, rs, LANES), f32),
                 pltpu.VMEM((chunks, np_, nx, nz, rs, LANES), bf16),
                 pltpu.VMEM((chunks, np_ * nx, nz, rs, LANES), bf16),
                 pltpu.VMEM((chunks, wide, nz, rs, LANES), bf16),
                 pltpu.VMEM((chunks, nz, rs, LANES), bf16),
-                dma((2,)), dma((chunks,)), dma((2,)), dma((chunks,)), dma(()), dma((chunks,)),
-                dma((2,)), dma((2,)), dma((2, nz)), dma((chunks,)), dma((chunks,)), dma((2,)),
-                dma((1 + nc * nx,)),
+                pltpu.VMEM((cs, nz, np_, nx, rs, LANES), bf16),
+                pltpu.VMEM((cs, half, half, np_, nx, rs, LANES), bf16),
+                pltpu.VMEM((cs, np_, nx, rs, LANES), bf16),
+                pltpu.VMEM((cs, nx, rs, LANES), bf16),
+                dma((4,)), dma((chunks,)), dma((cs,)), dma((3,)), dma((chunks,)), dma((2,)), dma((chunks,)),
+                dma((2,)), dma((2,)), dma((2, max(2, nz // 2))), dma((chunks,)), dma((chunks,)), dma((2,)),
+                dma((1 + nc // width * nx,)),
             ],
             compiler_params=pltpu.CompilerParams(
                 collective_id=0, has_side_effects=True, vmem_limit_bytes=VM * 1024 * 1024),

time: 46.4 us -> 40.1 us (0.86)
  Pallas kernels: 45.3 us -> 39 us
    pallas_call x1, Pallas kernels: 45.3 us -> 39 us  [local(): pl.pallas_call(functools.partial(kernel, np_, nx, nz, nc, ns), out_shape=...]
where the time goes in v3:
time: 40.1 us; the launch traced here: 39.9 us
  Pallas kernels  39 us (97%)
  local copies, waits for them, and re-layouts  0.97 us (2%)
    pallas_call x1, Pallas kernels, local(): pl.pallas_call(functools.partial(kernel, np_, nx, nz, nc, ns), out_shape=...  39 us
    unnamed x1, local copies, waits for them, and re-layouts  0.97 us

profile of v3, /device:TPU:0, one launch (start us, length us, event | category | flops | bytes accessed | tf_op | source)
XLA Modules:
  0.0 39.9 jit_solution(1222605311030285858)
XLA Ops:
  0.0 39.0 %shard_map.28 = bf16[256,2048]{1,0:T(8,128)(2,1)S(1)} custom-call(bf16[768,512]{1,0:T(8,128)(2,1)} %act_hbm.1, bf16[768,2048]{1,0:T(8,128)(2,1)} %cot_hbm.1), custom_call_target="tpu_custom_call" | custom-call | tf_op jit(solution)/shard_map/pallas_call | solution.py:382
  39.0 1.0 %copy.4 = bf16[256,2048]{1,0:T(8,128)(2,1)} copy(bf16[256,2048]{1,0:T(8,128)(2,1)S(1)} %shard_map.28) | data formatting | bytes 2097152

commit v4 on v3

--- a/solution.py
+++ b/solution.py
@@ -20,10 +20,9 @@
 SA = 2
 SB = 2
 OB = 1
-X_GATHER = "0"
-AHEAD = 4
-LAGS = (0, 4, 9, 14, 15, 19)
-XLAGS = (12, 17, 21)
+DIRECT = 3
+AHEAD = 5
+LAGS = (0, 4, 9, 12, 13, 18)
 
 
 def scale_and_offset(terms):
@@ -82,8 +81,8 @@
     def kind(k):
         return KINDS[k % len(KINDS)]
 
-    def x_gather(k):
-        return int(X_GATHER[k % len(X_GATHER)])
+    def direct(k):
+        return k >= chunks - DIRECT
 
     def remote(src, dst, ssem, rsem, peer):
         return pltpu.make_async_remote_copy(
@@ -106,17 +105,24 @@
         here = piece(k, zi, xi)
         remote(here, here, ssem, rsem, peer).start()
 
-    def gather_z(k, xi):
-        t = x_gather(k)
+    def gather_z(k):
         if nz > 1:
-            spread(k, z, xi, at_z(opposite), sgz.at[t], rf.at[k])
+            spread(k, z, x, at_z(opposite), sgz.at[0], rf.at[k])
         for q in range(1, half):
-            spread(k, z, xi, at_z(near(q)), sgz.at[t], rl.at[1] if t else rn.at[k])
+            spread(k, z, x, at_z(near(q)), sgz.at[0], rn.at[k])
 
     def gather_x(k, zi):
-        t = x_gather(k)
         for q in range(1, nx):
-            spread(k, zi, x, to_x(q), sgx.at[t], rn.at[k] if t else rl.at[0])
+            spread(k, zi, x, to_x(q), sgx.at[0], rl.at[0])
+
+    def gather_all(k):
+        for zo in range(nz):
+            for q in range(nx):
+                peer = {"dp": other(z, zo, nz) * nx + other(x, q, nx)}
+                if q:
+                    spread(k, z, x, peer, sgx.at[1], rl.at[1])
+                elif zo:
+                    spread(k, z, x, peer, sgz.at[1], rl.at[2])
 
     cs = [k for k in range(chunks) if kind(k) == "C"]
 
@@ -218,51 +224,42 @@
         for q in range(1, nz if kind(k) != "C" else 1):
             total = total + decode(zr[k, other(z, q, nz)], np_ * nx * terms)
         piece(k, z, x)[...] = (total / replicas).astype(out_ref.dtype)
-        if x_gather(k):
+        if direct(k):
+            gather_all(k)
+        else:
+            gather_z(k)
             gather_x(k, z)
-            gather_z(k, x)
-        else:
-            gather_z(k, x)
-            gather_x(k, z)
 
     def stage_near(k):
-        if x_gather(k):
-            arrived(enc.at[k, 0, pl.ds(0, nx - 1), 0], rn.at[k])
-            for q in range(1, nx):
-                gather_z(k, other(x, q, nx))
-        elif half > 1:
+        if half > 1 and not direct(k):
             arrived(enc.at[k, 0, 0, pl.ds(0, half - 1)], rn.at[k])
             for q in range(1, half):
                 gather_x(k, near(q))
 
-    def far_bytes(k):
-        return enc.at[k, 0, :, pl.ds(0, half)] if x_gather(k) else enc.at[k, 0, 0, pl.ds(0, half)]
-
     def stage_relay(k):
-        t = x_gather(k)
-        if half > 1:
+        if half > 1 and not direct(k):
             @pl.when(z == gateway)
             def _():
-                arrived(far_bytes(k), rf.at[k])
+                arrived(enc.at[k, 0, 0, pl.ds(0, half)], rf.at[k])
                 for j in range(half):
-                    for xi in [x] + [other(x, q, nx) for q in range(1, nx if t else 1)]:
-                        for q in range(1, half):
-                            spread(k, far + j, xi, at_z(near(q)), sr.at[t, q], rf.at[k])
+                    for q in range(1, half):
+                        spread(k, far + j, x, at_z(near(q)), sr.at[q], rf.at[k])
 
     def stage_far(k):
+        if nz == 1 or direct(k):
+            return
         if half > 1:
             @pl.when(z != gateway)
             def _():
-                arrived(far_bytes(k), rf.at[k])
-        elif nz > 1:
-            arrived(far_bytes(k), rf.at[k])
-        if nz > 1 and not x_gather(k):
-            for j in range(half):
-                gather_x(k, far + j)
+                arrived(enc.at[k, 0, 0, pl.ds(0, half)], rf.at[k])
+        else:
+            arrived(enc.at[k, 0, 0, pl.ds(0, half)], rf.at[k])
+        for j in range(half):
+            gather_x(k, far + j)
 
     def drain():
         a, b, c = (sum(kind(k) == t for k in range(chunks)) for t in "ABC")
-        g1 = sum(x_gather(k) for k in range(chunks))
+        g1 = sum(direct(k) for k in range(chunks))
         g0 = chunks - g1
         if a:
             sent(enc.at[pl.ds(0, a), pl.ds(0, np_ - 1)], s1.at[0])
@@ -278,27 +275,28 @@
             sent(enc.at[pl.ds(0, c), 0, pl.ds(0, nx - 1), 0], sz.at[1])
         if nz > 1 and a + b:
             sent(enc.at[pl.ds(0, a + b), 0, 0, pl.ds(0, nz - 1)], sz.at[0])
-        for t, g in ((0, g0), (1, g1)):
-            if not g:
-                continue
+        if g0:
             if nz > 1:
-                wide = enc.at[pl.ds(0, g), 0, :, pl.ds(0, half)] if t else enc.at[pl.ds(0, g), 0, 0, pl.ds(0, half)]
-                sent(wide, sgz.at[t])
+                group = enc.at[pl.ds(0, g0), 0, 0, pl.ds(0, half)]
+                sent(group, sgz.at[0])
                 if half > 1:
                     @pl.when(z == gateway)
                     def _():
                         for q in range(1, half):
-                            sent(wide, sr.at[t, q])
-            if t:
-                sent(enc.at[pl.ds(0, g), 0, pl.ds(0, nx - 1), 0], sgx.at[t])
-                if half > 1:
-                    arrived(enc.at[pl.ds(0, g), 0, :, pl.ds(0, half - 1)], rl.at[t])
-            else:
-                sent(enc.at[pl.ds(0, g), 0, pl.ds(0, nx - 1)], sgx.at[t])
-                arrived(enc.at[pl.ds(0, g), 0, pl.ds(0, nx - 1)], rl.at[t])
+                            sent(group, sr.at[q])
+            if nx > 1:
+                sent(enc.at[pl.ds(0, g0), 0, pl.ds(0, nx - 1)], sgx.at[0])
+                arrived(enc.at[pl.ds(0, g0), 0, pl.ds(0, nx - 1)], rl.at[0])
+        if g1:
+            if nz > 1:
+                sent(enc.at[pl.ds(0, g1), 0, 0, pl.ds(0, nz - 1)], sgz.at[1])
+                arrived(enc.at[pl.ds(0, g1), 0, 0, pl.ds(0, nz - 1)], rl.at[2])
+            if nx > 1:
+                sent(enc.at[pl.ds(0, g1), 0, pl.ds(0, nx - 1)], sgx.at[1])
+                arrived(enc.at[pl.ds(0, g1), 0, pl.ds(0, nx - 1)], rl.at[1])
 
     barrier = pltpu.get_barrier_semaphore()
-    peers = [to_pair(q) for q in range(1, np_)] + [to_x(q) for q in range(1, nx)] + [at_z(other(z, q, nz)) for q in range(1, nz)]
+    peers = [to_pair(q) for q in range(1, np_)] + [{"dp": other(dp, q, nz * nx)} for q in range(1, nz * nx)]
     for peer in peers:
         pl.semaphore_signal(barrier, inc=1, device_id=peer, device_id_type=pl.DeviceIdType.MESH)
 
@@ -335,7 +333,7 @@
 
     per = width * ns
     stages = [stage_first, stage_second, stage_third, stage_own, stage_near, stage_relay, stage_far, stage_pre]
-    lags = ((-AHEAD,) + LAGS, (-AHEAD,) + LAGS[:3] + XLAGS)
+    lags = (-AHEAD,) + LAGS
     events = []
     for k in range(chunks):
         if kind(k) == "C":
@@ -343,7 +341,7 @@
             slots = [CSLOTS[0]] + [slot + CSTEP * j for slot in CSLOTS[1:]]
         else:
             j = sum(kind(i) == kind(k) for i in range(k)) * (SA if kind(k) == "A" else SB) + (0 if kind(k) == "A" else OB)
-            slots = [RATE * j - AHEAD] + [j + lag for lag in lags[x_gather(k)][1:]]
+            slots = [RATE * j - AHEAD] + [j + lag for lag in lags[1:]]
         events += [(slot, -i, k) for i, slot in enumerate(slots)]
     events.sort()
     done = 0
@@ -398,7 +396,7 @@
                 pltpu.VMEM((cs, np_, nx, rs, LANES), bf16),
                 pltpu.VMEM((cs, nx, rs, LANES), bf16),
                 dma((4,)), dma((chunks,)), dma((cs,)), dma((3,)), dma((chunks,)), dma((2,)), dma((chunks,)),
-                dma((2,)), dma((2,)), dma((2, max(2, nz // 2))), dma((chunks,)), dma((chunks,)), dma((2,)),
+                dma((2,)), dma((2,)), dma((max(2, nz // 2),)), dma((chunks,)), dma((chunks,)), dma((3,)),
                 dma((1 + nc // width * nx,)),
             ],
             compiler_params=pltpu.CompilerParams(

time: 40.1 us -> 39.2 us (0.978)
  Pallas kernels: 39 us -> 38 us
    pallas_call x1, Pallas kernels: 39 us -> 38 us  [local(): pl.pallas_call(functools.partial(kernel, np_, nx, nz, nc, ns), out_shape=...]
where the time goes in v4:
time: 39.2 us; the launch traced here: 39 us
  Pallas kernels  38 us (97%)
  local copies, waits for them, and re-layouts  0.97 us (2%)
    pallas_call x1, Pallas kernels, local(): pl.pallas_call(functools.partial(kernel, np_, nx, nz, nc, ns), out_shape=...  38 us
    unnamed x1, local copies, waits for them, and re-layouts  0.97 us

profile of v4, /device:TPU:0, one launch (start us, length us, event | category | flops | bytes accessed | tf_op | source)
XLA Modules:
  0.0 39.0 jit_solution(13070690873494090589)
XLA Ops:
  0.0 38.0 %shard_map.28 = bf16[256,2048]{1,0:T(8,128)(2,1)S(1)} custom-call(bf16[768,512]{1,0:T(8,128)(2,1)} %act_hbm.1, bf16[768,2048]{1,0:T(8,128)(2,1)} %cot_hbm.1), custom_call_target="tpu_custom_call" | custom-call | tf_op jit(solution)/shard_map/pallas_call | solution.py:380
  38.0 1.0 %copy.4 = bf16[256,2048]{1,0:T(8,128)(2,1)} copy(bf16[256,2048]{1,0:T(8,128)(2,1)S(1)} %shard_map.28) | data formatting | bytes 2097152

commit v5 on v4

--- a/solution.py
+++ b/solution.py
@@ -295,11 +295,6 @@
                 sent(enc.at[pl.ds(0, g1), 0, pl.ds(0, nx - 1)], sgx.at[1])
                 arrived(enc.at[pl.ds(0, g1), 0, pl.ds(0, nx - 1)], rl.at[1])
 
-    barrier = pltpu.get_barrier_semaphore()
-    peers = [to_pair(q) for q in range(1, np_)] + [{"dp": other(dp, q, nz * nx)} for q in range(1, nz * nx)]
-    for peer in peers:
-        pl.semaphore_signal(barrier, inc=1, device_id=peer, device_id_type=pl.DeviceIdType.MESH)
-
     width = 2 if nc % 2 == 0 else 1
     groups = nc // width
     blocks = [(g, xi) for g in range(groups) for xi in range(nx)]
@@ -315,6 +310,12 @@
               for i, (g, xi) in enumerate(blocks)]
     for copy in loads:
         copy.start()
+
+    barrier = pltpu.get_barrier_semaphore()
+    peers = [to_pair(q) for q in range(1, np_)] + [{"dp": other(dp, q, nz * nx)} for q in range(1, nz * nx)]
+    for peer in peers:
+        pl.semaphore_signal(barrier, inc=1, device_id=peer, device_id_type=pl.DeviceIdType.MESH)
+
     loads[0].wait()
     act_t[...] = act_ref[...].T
 
@@ -396,7 +397,7 @@
                 pltpu.VMEM((cs, np_, nx, rs, LANES), bf16),
                 pltpu.VMEM((cs, nx, rs, LANES), bf16),
                 dma((4,)), dma((chunks,)), dma((cs,)), dma((3,)), dma((chunks,)), dma((2,)), dma((chunks,)),
-                dma((2,)), dma((2,)), dma((max(2, nz // 2),)), dma((chunks,)), dma((chunks,)), dma((3,)),
+                dma((2,)), dma((2,)), dma((max(2, nz // 2),)), dma((max(1, chunks - DIRECT),)), dma((max(1, chunks - DIRECT),)), dma((3,)),
                 dma((1 + nc // width * nx,)),
             ],
             compiler_params=pltpu.CompilerParams(

time: 39.2 us -> 39.2 us (level)
  no operation moved by 1% of the time
where the time goes in v5:
time: 39.2 us; the launch traced here: 39 us
  Pallas kernels  38 us (97%)
  local copies, waits for them, and re-layouts  0.97 us (2%)
    pallas_call x1, Pallas kernels, local(): pl.pallas_call(functools.partial(kernel, np_, nx, nz, nc, ns), out_shape=...  38 us
    unnamed x1, local copies, waits for them, and re-layouts  0.97 us

profile of v5, /device:TPU:0, one launch (start us, length us, event | category | flops | bytes accessed | tf_op | source)
XLA Modules:
  0.0 39.0 jit_solution(10465674962367551283)
XLA Ops:
  0.0 38.0 %shard_map.28 = bf16[256,2048]{1,0:T(8,128)(2,1)S(1)} custom-call(bf16[768,512]{1,0:T(8,128)(2,1)} %act_hbm.1, bf16[768,2048]{1,0:T(8,128)(2,1)} %cot_hbm.1), custom_call_target="tpu_custom_call" | custom-call | tf_op jit(solution)/shard_map/pallas_call | solution.py:381
  38.1 1.0 %copy.4 = bf16[256,2048]{1,0:T(8,128)(2,1)} copy(bf16[256,2048]{1,0:T(8,128)(2,1)S(1)} %shard_map.28) | data formatting | bytes 2097152
